TPU v7x, 32 devices: a whole 2x2x4 slice. The times are simulated.
32 devices in a mesh: mem: 4 (over z), state: 8 (over y, x, core).
Axes of the slice: x: 2, y: 2, z: 4, core: 2. Of those that a mesh axis runs over, the one named last changes fastest.
Arguments:
- anomalies: bfloat16 [64, 32, 32768], P('mem', None, 'state'), may hold values from -0.75 to 0.75
- alpha: bfloat16 [64, 32, 2048], P('mem', None, 'state'), may hold values from -6 to 6
- basis: bfloat16 [2048, 32768], P(None, 'state'), may hold values from -0.1875 to 0.1875
- gradient: bfloat16 [32, 32768], P(None, 'state'), may hold values from -6 to 6
- vertical_root: float32 [32, 32], replicated, may hold values from -1 to 1
- band_gain: float32 [16], replicated, may hold values from 0.25 to 2
- band: int32 [2048], P('state'), may hold values from 0 to 15
- order: int32 [64], replicated, may hold values from 0 to 63, each once
Outputs:
- increment: float32 [32, 32768], P(None, 'state')
- alpha_grad: float32 [64, 32, 2048], P('mem', None, 'state')
Inputs may be any that keep to these rules, and one draw needn't show every extreme that they name: `order`: a permutation: every member is named by exactly one slot.
All inputs are finite; a program needn't handle non-finite values.
Results may differ from a plain program's by a relative error of at most 0.0029.
Values may be sent and summed in bfloat16 or wider, within the bound.
A program may use at most 128 MiB of HBM per device.

v0:
```python
import jax
import jax.numpy as jnp
from jax import lax
from jax.sharding import PartitionSpec as P


def on_device(anomalies, alpha, basis, gradient, vertical_root, band_gain, band, order):
    high = lax.Precision.HIGHEST
    mem_count = lax.axis_size("mem")
    mem_rank = lax.axis_index("mem")
    member_dev, levels, columns = anomalies.shape
    mode_rows = alpha.shape[2]
    bands = band_gain.shape[0]
    onehot = (band[:, None] == jnp.arange(bands, dtype=jnp.int32)[None, :]).astype(jnp.float32)
    filter_gain = jnp.sum(onehot * band_gain[None, :], axis=1)
    coef = jnp.einsum("ab,jbk->jak", vertical_root, alpha.astype(jnp.float32), precision=high)
    coef = (coef * filter_gain[None, None, :]).astype(jnp.bfloat16)
    members = mem_rank * member_dev + jnp.arange(member_dev, dtype=jnp.int32)
    select = (order[None, :] == members[:, None]).astype(jnp.bfloat16)
    state_count = lax.axis_size("state")
    gathered = lax.all_gather(coef[None], ("mem", "state"), axis=0, tiled=True)
    blocks = gathered.reshape(mem_count, state_count, member_dev, levels, mode_rows)
    picked = jnp.einsum(
        "imj,msjlc->ilsc",
        select.reshape(member_dev, mem_count, member_dev),
        blocks,
        preferred_element_type=jnp.float32,
    )
    picked = picked.astype(jnp.bfloat16).reshape(member_dev * levels, state_count * mode_rows)
    member_field = jnp.dot(picked, basis, preferred_element_type=jnp.float32)
    partial_value = jnp.sum(
        anomalies.astype(jnp.float32) * member_field.reshape(member_dev, levels, columns), axis=0
    )
    increment = lax.psum(partial_value, "mem")
    weighted = (anomalies.astype(jnp.float32) * gradient.astype(jnp.float32)[None]).astype(
        jnp.bfloat16
    )
    weighted = weighted.reshape(member_dev * levels, columns)
    projected = lax.psum_scatter(
        lax.dot_general(
            basis, weighted, (((1,), (1,)), ((), ())), preferred_element_type=jnp.float32
        ),
        "state",
        scatter_dimension=0,
        tiled=True,
    )
    member_grad = jnp.einsum(
        "ab,kma->mbk",
        vertical_root,
        projected.reshape(mode_rows, member_dev, levels),
        precision=high,
    )
    member_grad = member_grad * filter_gain[None, None, :]
    placed = jnp.einsum("ij,ibk->jbk", select.astype(jnp.float32), member_grad, precision=high)
    outgoing = placed.reshape(mem_count, member_dev, levels, mode_rows)
    incoming = lax.all_to_all(outgoing, "mem", split_axis=0, concat_axis=0, tiled=True)
    alpha_grad = jnp.sum(incoming, axis=0)
    return (increment, alpha_grad)


def solution(mesh):
    return jax.shard_map(
        on_device,
        mesh=mesh,
        in_specs=(
            P("mem", None, "state"),
            P("mem", None, "state"),
            P(None, "state"),
            P(None, "state"),
            P(),
            P(),
            P("state"),
            P(),
        ),
        out_specs=(P(None, "state"), P("mem", None, "state")),
        check_vma=False,
    )
```

profile of v0, /device:TPU:0, one launch (start us, length us, event | category | flops | bytes accessed | tf_op | source)
XLA Modules:
  0.0 206.5 jit_solution(10233362292895392196)
XLA Ops:
  8.0 0.0 reduce-scatter.2.cloned.1.call-start
  8.1 1.0 convert_element_type.31
  9.1 3.3 %fusion.3 = bf16[16,32,4096]{2,1,0:T(8,128)(2,1)S(1)} fusion(bf16[16,32,4096]{2,1,0:T(8,128)(2,1)} %param.8, f32[32,4096]{1,0:T(8,128)S(1)} %convert_element_type.31), kind=kLoop, calls=%fused_computation.5 | loop fusion | flops 6291456 | bytes 8912896 | tf_op jit(solution)/shard_map/convert_element_type | solution.py:35
  12.4 13.7 %convolution_bitcast_fusion = f32[2048,512]{0,1:T(8,128)} fusion(bf16[512,4096]{1,0:T(8,128)(2,1)S(1)} %bitcast.44, bf16[2048,4096]{1,0:T(8,128)(2,1)} %param.10), kind=kOutput, calls=%fused_computation.9 | convolution fusion | flops 8589934592 | bytes 25165824 | tf_op jit(solution)/shard_map/dot_general | solution.py:40
  26.2 0.0 reduce-scatter.2.cloned.1.call-update
  26.2 0.0 all-gather.3.cloned.1.call-start
  26.2 0.6 copy-done.3
  26.8 0.1 select_reduce_fusion
  26.9 1.1 fusion.15
  28.0 0.1 eq.38
  28.1 52.4 %reduce-scatter.2.cloned.1.call-done = f32[256,512]{0,1:T(8,128)} async-done(((f32[2048,512]{0,1:T(8,128)}), f32[256,512]{0,1:T(8,128)}) %reduce-scatter.2.cloned.1.call-update) | async-done | bytes 524304 | tf_op jit(solution)/shard_map/reduce_scatter | solution.py:39
  80.5 1.7 fusion.13
  82.2 1.2 fusion.16
  83.3 1.6 copy.30
  84.9 4.6 %all-to-all-start = ((f32[4,16,32,256]{3,1,2,0:T(8,128)}), f32[4,16,32,256]{3,1,2,0:T(8,128)S(1)}, u32[]{:S(2)}, u32[]{:S(2)}) async-start(f32[4,16,32,256]{3,1,2,0:T(8,128)} %copy.30), calls=%async_computation.1 | async-start | bytes 4194304 | tf_op jit(solution)/shard_map/all_to_all | solution.py:56
  89.5 41.0 %all-gather.3.cloned.1.call-done = bf16[512,32,256]{2,1,0:T(8,128)(2,1)} async-done(((bf16[16,32,256]{2,1,0:T(8,128)(2,1)}), bf16[512,32,256]{2,1,0:T(8,128)(2,1)}) %all-gather.3.cloned.1.call-update) | async-done | bytes 8388624 | tf_op jit(solution)/shard_map/all_gather | solution.py:21
  130.5 8.1 %fusion.10 = bf16[16,32,8,256]{3,0,1,2:T(8,128)(2,1)S(1)} fusion(bf16[4,8,16,32,256]{4,3,2,1,0:T(8,128)(2,1)} %bitcast.46, s32[4,16]{1,0:T(4,128)S(1)} %eq.38, s32[16]{0:T(128)S(1)} %iota_add_fusion), kind=kOutput, calls=%fused_computation.10 | convolution fusion | flops 135267328 | bytes 10486080 | tf_op jit(solution)/shard_map/imj,msjlc->ilsc/dot_general | solution.py:23
  138.6 2.5 %copy.27 = bf16[16,32,8,256]{3,2,1,0:T(8,128)(2,1)} copy(bf16[16,32,8,256]{3,0,1,2:T(8,128)(2,1)S(1)} %fusion.10) | data formatting | bytes 4194304 | tf_op jit(solution)/shard_map/convert_element_type | solution.py:29
  141.1 4.2 %dot_general.24 = bf16[16,32,2048]{2,1,0:T(8,128)(2,1)} reshape(bf16[16,32,8,256]{3,2,1,0:T(8,128)(2,1)} %copy.27) | data formatting | bytes 4194304 | tf_op jit(solution)/shard_map/dot_general | solution.py:30
  145.3 14.4 %fusion.2 = f32[32,4096]{1,0:T(8,128)} fusion(bf16[16,32,4096]{2,1,0:T(8,128)(2,1)} %param.8, bf16[16,32,2048]{2,1,0:T(8,128)(2,1)} %dot_general.24, bf16[2048,4096]{1,0:T(8,128)(2,1)} %param.10), kind=kOutput, calls=%fused_computation.4 | convolution fusion | flops 8596094976 | bytes 23592960 | tf_op jit(solution)/shard_map/dot_general | solution.py:30
  159.8 0.2 reduce_sum.29
  160.1 1.1 copy.32
  161.2 36.1 %all-reduce.2.cloned.1.call-done = f32[32,4096]{1,0:T(8,128)} async-done(((f32[32,4096]{1,0:T(8,128)}), f32[32,4096]{1,0:T(8,128)}) %all-reduce.2.cloned.1.call-update) | async-done | bytes 524304 | tf_op jit(solution)/shard_map/psum | solution.py:34
  197.2 1.9 copy.47
  (14 shorter events, 0.1 us)
Async XLA Ops:
  8.0 18.9 %copy-start = (bf16[16,32,256]{2,1,0:T(8,128)(2,1)S(1)}, bf16[16,32,256]{2,1,0:T(8,128)(2,1)}, u32[]{:S(2)}) copy-start(bf16[16,32,256]{2,1,0:T(8,128)(2,1)} %param.9) | copy-start | bytes 786436
  8.0 72.5 %reduce-scatter.2.cloned.1.call-start = ((), (), s32[]{:S(2)}) async-start(), calls=%async_computation.3 | async-start | bytes 4718592 | tf_op jit(solution)/shard_map/reduce_scatter | solution.py:39
  26.2 0.7 copy-start.3
  26.2 0.7 copy-start.4
  26.2 0.8 copy-start.1
  26.2 1.9 copy-start.2
  26.2 104.3 %all-gather.3.cloned.1.call-start = ((), (), s32[]{:S(2)}) async-start(), calls=%async_computation.4 | async-start | bytes 8650752 | tf_op jit(solution)/shard_map/all_gather | solution.py:21
  84.9 74.9 %all-to-all-start = ((f32[4,16,32,256]{3,1,2,0:T(8,128)}), f32[4,16,32,256]{3,1,2,0:T(8,128)S(1)}, u32[]{:S(2)}, u32[]{:S(2)}) async-start(f32[4,16,32,256]{3,1,2,0:T(8,128)} %copy.30), calls=%async_computation.1 | async-start | bytes 4194304 | tf_op jit(solution)/shard_map/all_to_all | solution.py:56
  89.5 107.7 %all-reduce.2.cloned.1.call-start = ((), (), s32[]{:S(2)}) async-start(), calls=%async_computation.2 | async-start | bytes 1048576 | tf_op jit(solution)/shard_map/psum | solution.py:34
Sparse Core Ops, SparseCore 0:
  26.3 54.1 reduce-scatter.1
Sparse Core Ops, SparseCore 1:
  30.1 100.3 all-gather.2
  159.9 37.3 all-reduce.1
where the time goes:
time: 207 us
  waiting for transfers between devices  129 us (62%)
  matrix products  40.2 us (19%)
  between operations  15.6 us (8%)
  local copies, waits for them, and re-layouts  11.9 us (6%)
  starting transfers between devices  4.71 us (2%)
  other arithmetic  4.69 us (2%)
    reduce_scatter x1, waiting for transfers between devices, on_device(): lax.psum_scatter(lax.dot_general(basis, weighted, (((1,), (1,)), ((), ())...  52.4 us
    all_gather x1, waiting for transfers between devices, on_device(): gathered = lax.all_gather(coef[None], ('mem', 'state'), axis=0, tiled=True)  41 us
    psum x1, waiting for transfers between devices, on_device(): increment = lax.psum(partial_value, 'mem')  36.1 us
    dot_general x1, matrix products, on_device(): member_field = jnp.dot(picked, basis, preferred_element_type=jnp.float32)  14.4 us
    dot_general x1, matrix products, on_device(): lax.dot_general(basis, weighted, (((1,), (1,)), ((), ())), preferred_elem...  13.7 us
    dot_general x1, matrix products, on_device(): jnp.einsum('imj,msjlc->ilsc', select.reshape(member_dev, mem_count, membe...  8.11 us
    all_to_all x1, starting transfers between devices, on_device(): lax.all_to_all(outgoing, 'mem', split_axis=0, concat_axis=0, tiled=True)  4.62 us
    dot_general x1, local copies, waits for them, and re-layouts, on_device(): member_field = jnp.dot(picked, basis, preferred_element_type=jnp.float32)  4.19 us
  transfers between devices with their start and end apart: 4, of which 3 were waited for; matrix products, arithmetic and copies ran while one was open for 18% of the time, Pallas kernels for 0%

commit v1 on v0

--- a/solution.py
+++ b/solution.py
@@ -31,7 +31,8 @@
     partial_value = jnp.sum(
         anomalies.astype(jnp.float32) * member_field.reshape(member_dev, levels, columns), axis=0
     )
-    increment = lax.psum(partial_value, "mem")
+    parts = lax.all_gather(partial_value, "mem")
+    increment = jnp.sum(parts, axis=0)
     weighted = (anomalies.astype(jnp.float32) * gradient.astype(jnp.float32)[None]).astype(
         jnp.bfloat16
     )

time: 207 us -> 214 us (1.034)
  waiting for transfers between devices: 129 us -> 136 us
  other arithmetic: 4.69 us -> 7.23 us
    all_gather x0 -> x1, waiting for transfers between devices: none -> 42.8 us  [on_device(): parts = lax.all_gather(partial_value, 'mem')]
    psum x1 -> x0, waiting for transfers between devices: 36.1 us -> none  [on_device(): increment = lax.psum(partial_value, 'mem')]
    reduce_sum x0 -> x1, other arithmetic: none -> 2.55 us  [on_device(): increment = jnp.sum(parts, axis=0)]
  transfers between devices with their start and end apart: 4 -> 4, of which waited for: 3 -> 3; matrix products, arithmetic and copies ran while one was open for 18% -> 17% of each run, Pallas kernels for 0% -> 0%
where the time goes in v1:
time: 214 us
  waiting for transfers between devices  136 us (64%)
  matrix products  40.2 us (19%)
  between operations  15.6 us (7%)
  local copies, waits for them, and re-layouts  10.1 us (5%)
  other arithmetic  7.23 us (3%)
  starting transfers between devices  4.71 us (2%)
    reduce_scatter x1, waiting for transfers between devices, on_device(): lax.psum_scatter(lax.dot_general(basis, weighted, (((1,), (1,)), ((), ())...  52.4 us
    all_gather x1, waiting for transfers between devices, on_device(): parts = lax.all_gather(partial_value, 'mem')  42.8 us
    all_gather x1, waiting for transfers between devices, on_device(): gathered = lax.all_gather(coef[None], ('mem', 'state'), axis=0, tiled=True)  41 us
    dot_general x1, matrix products, on_device(): member_field = jnp.dot(picked, basis, preferred_element_type=jnp.float32)  14.4 us
    dot_general x1, matrix products, on_device(): lax.dot_general(basis, weighted, (((1,), (1,)), ((), ())), preferred_elem...  13.7 us
    dot_general x1, matrix products, on_device(): jnp.einsum('imj,msjlc->ilsc', select.reshape(member_dev, mem_count, membe...  8.11 us
    all_to_all x1, starting transfers between devices, on_device(): lax.all_to_all(outgoing, 'mem', split_axis=0, concat_axis=0, tiled=True)  4.62 us
  transfers between devices with their start and end apart: 4, of which 3 were waited for; matrix products, arithmetic and copies ran while one was open for 17% of the time, Pallas kernels for 0%

profile of v1, /device:TPU:0, one launch (start us, length us, event | category | flops | bytes accessed | tf_op | source)
XLA Modules:
  0.0 213.9 jit_solution(15006399671041799905)
XLA Ops:
  8.0 0.0 reduce-scatter.2.cloned.1.call-start
  8.1 1.0 convert_element_type.31
  9.1 3.3 %fusion.3 = bf16[16,32,4096]{2,1,0:T(8,128)(2,1)S(1)} fusion(bf16[16,32,4096]{2,1,0:T(8,128)(2,1)} %param.8, f32[32,4096]{1,0:T(8,128)S(1)} %convert_element_type.31), kind=kLoop, calls=%fused_computation.5 | loop fusion | flops 6291456 | bytes 8912896 | tf_op jit(solution)/shard_map/convert_element_type | solution.py:36
  12.4 13.7 %convolution_bitcast_fusion = f32[2048,512]{0,1:T(8,128)} fusion(bf16[512,4096]{1,0:T(8,128)(2,1)S(1)} %bitcast.45, bf16[2048,4096]{1,0:T(8,128)(2,1)} %param.10), kind=kOutput, calls=%fused_computation.9 | convolution fusion | flops 8589934592 | bytes 25165824 | tf_op jit(solution)/shard_map/dot_general | solution.py:41
  26.2 0.0 reduce-scatter.2.cloned.1.call-update
  26.2 0.0 all-gather.5.cloned.1.call-start
  26.2 0.6 copy-done.3
  26.8 0.1 select_reduce_fusion
  26.9 1.1 fusion.15
  28.0 0.1 eq.38
  28.1 52.4 %reduce-scatter.2.cloned.1.call-done = f32[256,512]{0,1:T(8,128)} async-done(((f32[2048,512]{0,1:T(8,128)}), f32[256,512]{0,1:T(8,128)}) %reduce-scatter.2.cloned.1.call-update) | async-done | bytes 524304 | tf_op jit(solution)/shard_map/reduce_scatter | solution.py:40
  80.5 1.7 fusion.13
  82.2 1.2 fusion.16
  83.3 1.6 copy.30
  84.9 4.6 %all-to-all-start = ((f32[4,16,32,256]{3,1,2,0:T(8,128)}), f32[4,16,32,256]{3,1,2,0:T(8,128)S(1)}, u32[]{:S(2)}, u32[]{:S(2)}) async-start(f32[4,16,32,256]{3,1,2,0:T(8,128)} %copy.30), calls=%async_computation.1 | async-start | bytes 4194304 | tf_op jit(solution)/shard_map/all_to_all | solution.py:57
  89.5 41.0 %all-gather.5.cloned.1.call-done = bf16[512,32,256]{2,1,0:T(8,128)(2,1)} async-done(((bf16[16,32,256]{2,1,0:T(8,128)(2,1)}), bf16[512,32,256]{2,1,0:T(8,128)(2,1)}) %all-gather.5.cloned.1.call-update) | async-done | bytes 8388624 | tf_op jit(solution)/shard_map/all_gather | solution.py:21
  130.5 8.1 %fusion.10 = bf16[16,32,8,256]{3,0,1,2:T(8,128)(2,1)S(1)} fusion(bf16[4,8,16,32,256]{4,3,2,1,0:T(8,128)(2,1)} %bitcast.48, s32[4,16]{1,0:T(4,128)S(1)} %eq.38, s32[16]{0:T(128)S(1)} %iota_add_fusion), kind=kOutput, calls=%fused_computation.10 | convolution fusion | flops 135267328 | bytes 10486080 | tf_op jit(solution)/shard_map/imj,msjlc->ilsc/dot_general | solution.py:23
  138.6 2.5 %copy.27 = bf16[16,32,8,256]{3,2,1,0:T(8,128)(2,1)} copy(bf16[16,32,8,256]{3,0,1,2:T(8,128)(2,1)S(1)} %fusion.10) | data formatting | bytes 4194304 | tf_op jit(solution)/shard_map/convert_element_type | solution.py:29
  141.1 4.2 %dot_general.24 = bf16[16,32,2048]{2,1,0:T(8,128)(2,1)} reshape(bf16[16,32,8,256]{3,2,1,0:T(8,128)(2,1)} %copy.27) | data formatting | bytes 4194304 | tf_op jit(solution)/shard_map/dot_general | solution.py:30
  145.3 14.4 %fusion.2 = f32[32,4096]{1,0:T(8,128)} fusion(bf16[16,32,4096]{2,1,0:T(8,128)(2,1)} %param.8, bf16[16,32,2048]{2,1,0:T(8,128)(2,1)} %dot_general.24, bf16[2048,4096]{1,0:T(8,128)(2,1)} %param.10), kind=kOutput, calls=%fused_computation.4 | convolution fusion | flops 8596094976 | bytes 23592960 | tf_op jit(solution)/shard_map/dot_general | solution.py:30
  159.8 0.2 reduce_sum.39
  160.1 1.1 copy.32
  161.2 42.8 %all-gather.7.cloned.1.call-done = f32[128,4096]{1,0:T(8,128)} async-done(((f32[32,4096]{1,0:T(8,128)}), f32[128,4096]{1,0:T(8,128)}) %all-gather.7.cloned.1.call-update) | async-done | bytes 2097168 | tf_op jit(solution)/shard_map/all_gather | solution.py:34
  204.0 2.5 %reduce_sum.38 = f32[32,4096]{1,0:T(8,128)} reduce(f32[4,32,4096]{2,1,0:T(8,128)} %bitcast.46, f32[]{:T(128)} %constant.3.clone.1), dimensions={0}, to_apply=%region_2.0 | reduce | flops 393216 | bytes 2621444 | tf_op jit(solution)/shard_map/reduce_sum | solution.py:35
  (14 shorter events, 0.1 us)
Async XLA Ops:
  8.0 18.9 %copy-start = (bf16[16,32,256]{2,1,0:T(8,128)(2,1)S(1)}, bf16[16,32,256]{2,1,0:T(8,128)(2,1)}, u32[]{:S(2)}) copy-start(bf16[16,32,256]{2,1,0:T(8,128)(2,1)} %param.9) | copy-start | bytes 786436
  8.0 72.5 %reduce-scatter.2.cloned.1.call-start = ((), (), s32[]{:S(2)}) async-start(), calls=%async_computation.2 | async-start | bytes 4718592 | tf_op jit(solution)/shard_map/reduce_scatter | solution.py:40
  26.2 0.7 copy-start.3
  26.2 0.7 copy-start.4
  26.2 0.8 copy-start.1
  26.2 1.9 copy-start.2
  26.2 104.3 %all-gather.5.cloned.1.call-start = ((), (), s32[]{:S(2)}) async-start(), calls=%async_computation.3 | async-start | bytes 8650752 | tf_op jit(solution)/shard_map/all_gather | solution.py:21
  84.9 74.9 %all-to-all-start = ((f32[4,16,32,256]{3,1,2,0:T(8,128)}), f32[4,16,32,256]{3,1,2,0:T(8,128)S(1)}, u32[]{:S(2)}, u32[]{:S(2)}) async-start(f32[4,16,32,256]{3,1,2,0:T(8,128)} %copy.30), calls=%async_computation.1 | async-start | bytes 4194304 | tf_op jit(solution)/shard_map/all_to_all | solution.py:57
  89.5 114.5 %all-gather.7.cloned.1.call-start = ((), (), s32[]{:S(2)}) async-start(), calls=%async_computation.4 | async-start | bytes 2621440 | tf_op jit(solution)/shard_map/all_gather | solution.py:34
Sparse Core Ops, SparseCore 0:
  26.3 54.1 reduce-scatter.1
Sparse Core Ops, SparseCore 1:
  30.1 100.3 all-gather.4
  159.9 44.0 all-gather.6
